TPU v7x, 32 devices: a whole 2x2x4 slice. The times are simulated.
32 devices in a mesh: row: 8 (over z, core), col: 4 (over y, x).
Axes of the slice: x: 2, y: 2, z: 4, core: 2. Of those that a mesh axis runs over, the one named last changes fastest.
Arguments:
- train_weight: bfloat16 [4, 4608, 2048], P(None, 'row', 'col')
- src_map: int32 [16], replicated, may hold values from 0 to 15, as said below
- tgt_map: int32 [16], replicated, may hold values from 0 to 15, as said below
- probe: bfloat16 [4096, 4608], P('row'), may hold values from -6 to 6
Outputs:
- codes: bfloat16 [4, 4608, 2048], P(None, None, 'col')
- peaks: float32 [4, 16], P(None, 'col')
- checked: bfloat16 [4, 4096, 2048], P(None, 'row', 'col')
Inputs may be any that keep to these rules, and one draw needn't show every extreme that they name: src_map is a permutation of 0 to 15. tgt_map is a permutation of 0 to 15. Call column k the slots k * 4 to (k + 1) * 4 - 1 of a map, and let C = 4. There are three different offsets a, b, c in 0 to C - 1, the same for every column, of which one is C / 2 and one is C - 1: the heads of training column k stand in serving columns (k - a) mod C (2 of them), (k - b) mod C (one) and (k - c) mod C (one).
All inputs are finite; a program needn't handle non-finite values. Where the computation divides by a largest or mean magnitude, that divisor is 1e-20 or more.
Results may differ from a plain program's by a relative error of at most 0.0049.
Values may be sent and summed in bfloat16 or wider, within the bound.
A program may use at most 128 MiB of HBM per device.

v0:
```python
import jax
import jax.numpy as jnp
from jax import lax
from jax.sharding import PartitionSpec as P

HDIM = 128


def per_device(train_weight, src_map, tgt_map, probe):
    col_count = lax.axis_size("col")
    heads_all = src_map.shape[0]
    per_col = heads_all // col_count
    layers = train_weight.shape[0]
    rows_here = train_weight.shape[1]
    column = lax.axis_index("col")
    wanted = lax.dynamic_slice(tgt_map, (column * per_col,), (per_col,))
    shard_piece = lax.all_gather(train_weight, "col", axis=2, tiled=True)
    count = shard_piece.shape[2] // HDIM
    selector = (src_map[:, None] == wanted[None, :]).astype(jnp.bfloat16)
    picked = jnp.einsum(
        "ldpe,ph->ldhe",
        shard_piece.reshape(layers, rows_here, count, HDIM),
        selector,
        preferred_element_type=jnp.float32,
    )
    block_part = picked.astype(jnp.bfloat16)
    joined = lax.all_gather(
        block_part.reshape(layers, rows_here, per_col * HDIM), "row", axis=1, tiled=True
    )
    joined_four = joined.reshape(layers, -1, per_col, HDIM)
    peaks = jnp.max(jnp.abs(joined_four.astype(jnp.float32)), axis=(1, 3))
    codes = (joined_four.astype(jnp.float32) / (peaks[:, None, :, None] + 1e-06)).astype(
        jnp.bfloat16
    )
    codes = codes.reshape(layers, -1, per_col * HDIM)
    projected = jnp.einsum("td,lde->lte", probe, codes, preferred_element_type=jnp.float32)
    checked = (projected * jnp.repeat(peaks, HDIM, axis=1)[:, None, :]).astype(jnp.bfloat16)
    return (codes, peaks, checked)


def solution(mesh):
    in_specs = (P(None, "row", "col"), P(), P(), P("row", None))
    out_specs = (P(None, None, "col"), P(None, "col"), P(None, "row", "col"))
    return jax.shard_map(
        per_device, mesh=mesh, in_specs=in_specs, out_specs=out_specs, check_vma=False
    )
```

profile of v0, /device:TPU:5, one launch (start us, length us, event | category | flops | bytes accessed | tf_op | source)
XLA Modules:
  0.0 344.1 jit_solution(16270182239731560487)
XLA Ops:
  7.2 0.0 all-gather.3.cloned.1.call-start
  7.2 0.7 all-gather.3.cloned.1.call-update
  7.9 0.0 all-gather.5.cloned.1.call-start
  7.9 0.7 dynamic_slice.3
  8.7 98.3 %all-gather.3.cloned.1.call-done = bf16[4,576,2048]{2,1,0:T(8,128)(2,1)} async-done(((bf16[4,576,512]{2,1,0:T(8,128)(2,1)}), bf16[4,576,2048]{2,1,0:T(8,128)(2,1)}) %all-gather.3.cloned.1.call-update) | async-done | bytes 9437200 | tf_op jit(solution)/shard_map/all_gather | solution.py:17
  106.9 0.0 copy-start.1
  106.9 11.0 %copy.13 = bf16[288,8,16,128]{3,2,1,0:T(8,128)(2,1)} copy(bf16[288,8,16,128]{3,1,2,0:T(8,128)(2,1)} %bitcast.38) | data formatting | bytes 18874368
  117.9 0.0 copy-done.1
  117.9 5.1 %convert_bitcast_fusion = bf16[4,576,4,128]{3,2,1,0:T(4,128)(2,1)S(1)} fusion(s32[16]{0:T(128)S(1)} %copy-done.1, s32[4]{0:T(128)S(1)} %dynamic_slice.3, bf16[4,576,16,128]{3,2,1,0:T(8,128)(2,1)} %bitcast.37), kind=kOutput, calls=%fused_computation.9 | convolution fusion | flops 38928448 | bytes 11796560 | tf_op jit(solution)/shard_map/ldpe,ph->ldhe/dot_general | solution.py:20
  123.1 2.3 reshape.24
  125.4 0.0 all-gather.5.cloned.1.call-update
  125.4 169.0 %all-gather.5.cloned.1.call-done = bf16[4,4608,512]{2,1,0:T(8,128)(2,1)} async-done(((bf16[4,576,512]{2,1,0:T(8,128)(2,1)}), bf16[4,4608,512]{2,1,0:T(8,128)(2,1)}) %all-gather.5.cloned.1.call-update) | async-done | bytes 18874384 | tf_op jit(solution)/shard_map/all_gather | solution.py:27
  294.4 7.4 %fusion = f32[4,512]{1,0:T(4,128)S(1)} fusion(bf16[4,4608,512]{2,1,0:T(8,128)(2,1)} %all-gather.5.cloned.1.call-done), kind=kLoop, calls=%fused_computation.2 | loop fusion | flops 28309504 | bytes 18882560 | tf_op jit(solution)/shard_map/reduce_max | solution.py:31
  301.8 0.1 reduce_max.18
  301.9 0.0 copy-start
  301.9 0.1 broadcast_bitcast_fusion
  302.0 0.1 broadcast_bitcast_fusion.1
  302.1 17.7 %fusion.1 = bf16[4,4608,512]{2,1,0:T(8,128)(2,1)} fusion(bf16[4,4608,512]{2,1,0:T(8,128)(2,1)} %all-gather.5.cloned.1.call-done, f32[4,512]{1,0:T(4,128)S(1)} %bitcast.39), kind=kLoop, calls=%fused_computation.3 | loop fusion | flops 28311552 | bytes 37756928 | tf_op jit(solution)/shard_map/convert_element_type | solution.py:32
  319.7 0.0 copy-done
  319.7 15.2 %fusion.10 = bf16[4,512,512]{1,2,0:T(8,128)(2,1)S(1)} fusion(f32[4,512]{1,0:T(4,128)S(1)} %bitcast.40, bf16[4,4608,512]{2,1,0:T(8,128)(2,1)} %fusion.1, bf16[512,4608]{1,0:T(8,128)(2,1)} %param.7), kind=kOutput, calls=%fused_computation.10 | convolution fusion | flops 9665773568 | bytes 25698304 | tf_op jit(solution)/shard_map/td,lde->lte/dot_general | solution.py:36
  334.9 2.4 copy.10
  (4 shorter events, 0.0 us)
Async XLA Ops:
  7.2 99.8 %all-gather.3.cloned.1.call-start = ((), (), s32[]{:S(2)}) async-start(), calls=%async_computation | async-start | bytes 11796480 | tf_op jit(solution)/shard_map/all_gather | solution.py:17
  7.9 286.5 %all-gather.5.cloned.1.call-start = ((), (), s32[]{:S(2)}) async-start(), calls=%async_computation.1 | async-start | bytes 21233664 | tf_op jit(solution)/shard_map/all_gather | solution.py:27
  106.9 11.0 %copy-start.1 = (s32[16]{0:T(128)S(1)}, s32[16]{0:T(128)}, u32[]{:S(2)}) copy-start(s32[16]{0:T(128)} %param.5) | copy-start | bytes 196
  301.9 17.8 %copy-start = (f32[4,4]{1,0:T(4,128)}, f32[4,4]{1,0:T(4,128)S(1)}, u32[]{:S(2)}) copy-start(f32[4,4]{1,0:T(4,128)S(1)} %reduce_max.18) | copy-start | bytes 196
Sparse Core Ops, SparseCore 0:
  9.8 97.0 all-gather.2
  125.5 168.8 all-gather.4
where the time goes:
time: 346 us; the launch traced here: 344 us
  waiting for transfers between devices  268 us (77%)
  other arithmetic  25.1 us (7%)
  matrix products  20.3 us (6%)
  local copies, waits for them, and re-layouts  16.6 us (5%)
  between operations  14.1 us (4%)
    all_gather x1, waiting for transfers between devices, per_device(): lax.all_gather(block_part.reshape(layers, rows_here, per_col * HDIM), 'ro...  169 us
    all_gather x1, waiting for transfers between devices, per_device(): shard_piece = lax.all_gather(train_weight, 'col', axis=2, tiled=True)  98.3 us
    convert_element_type x1, other arithmetic, per_device(): (joined_four.astype(jnp.float32) / (peaks[:, None, :, None] + 1e-06)).ast...  17.7 us
    dot_general x1, matrix products, per_device(): jnp.einsum('td,lde->lte', probe, codes, preferred_element_type=jnp.float32)  15.2 us
    unnamed x10, local copies, waits for them, and re-layouts  13.5 us
    reduce_max x2, other arithmetic, per_device(): peaks = jnp.max(jnp.abs(joined_four.astype(jnp.float32)), axis=(1, 3))  7.46 us
  transfers between devices with their start and end apart: 2, of which 2 were waited for; matrix products, arithmetic and copies ran while one was open for 0% of the time, Pallas kernels for 0%

commit v1 on v0

v1 whole, which is shorter than its diff:
```python
import functools

import jax
import jax.numpy as jnp
from jax import lax
from jax.experimental import pallas as pl
from jax.experimental.pallas import tpu as pltpu
from jax.sharding import PartitionSpec as P

HDIM = 128
CORES = 2
TILE = 16
KSTEP = 512
MESH = pl.DeviceIdType.MESH


def pieces_of(rows, most):
    for count in range(most, 0, -1):
        if rows % (TILE * count) == 0:
            return count
    return 1


def chunk_list(layers, rows):
    out = []
    for layer in range(layers):
        count = pieces_of(rows, 4 if layer == 0 else 2)
        size = rows // count
        for i in range(count):
            out.append((layer, i * size, size))
    return out


def kernel(
    chunks, zs, cols, source_ref, w_ref, probe_ref, codes_ref, checked_ref, peaks_ref,
    full, cbuf, pbuf, chk, guard,
    csend, crecv, zsend, zrecv, local, outsem, *raws,
):
    layers, heads, width, _ = full.shape
    rows = w_ref.shape[1]
    tokens = pbuf.shape[0]
    me = lax.axis_index("row")
    mycol = lax.axis_index("col")
    z = me // CORES
    core = me % CORES
    partner = z * CORES + (1 - core)
    has_down = z > 0
    has_up = z < zs - 1

    barrier = pltpu.get_barrier_semaphore()
    for o in range(1, cols):
        pl.semaphore_signal(
            barrier, inc=1, device_id={"col": lax.rem(mycol + o, cols)}, device_id_type=MESH
        )
    pl.semaphore_signal(barrier, inc=1, device_id={"row": partner}, device_id_type=MESH)

    @pl.when(has_down)
    def _():
        pl.semaphore_signal(barrier, inc=1, device_id={"row": me - CORES}, device_id_type=MESH)

    @pl.when(has_up)
    def _():
        pl.semaphore_signal(barrier, inc=1, device_id={"row": me + CORES}, device_id_type=MESH)

    pl.semaphore_wait(barrier, cols + has_down.astype(jnp.int32) + has_up.astype(jnp.int32))

    def raw_at(g, owner, head):
        return raws[g].at[owner * heads + head]

    def col_copy(g, owner, target, head):
        layer, r0, size = chunks[g]
        return pltpu.make_async_remote_copy(
            src_ref=w_ref.at[layer, pl.ds(r0, size), pl.ds(head * HDIM, HDIM)],
            dst_ref=raw_at(g, owner, head),
            send_sem=csend.at[g, target, head],
            recv_sem=crecv.at[g, owner, head],
            device_id={"col": target},
            device_id_type=MESH,
        )

    def own_copy(g, head):
        layer, r0, size = chunks[g]
        return pltpu.make_async_copy(
            w_ref.at[layer, pl.ds(r0, size), pl.ds(head * HDIM, HDIM)],
            raw_at(g, mycol, head),
            local.at[g, head],
        )

    for g in range(len(chunks)):
        for head in range(heads):
            for o in range(1, cols):
                col_copy(g, mycol, lax.rem(mycol + o, cols), head).start()
            own_copy(g, head).start()
    probe_copy = pltpu.make_async_copy(probe_ref, pbuf, outsem.at[0])
    probe_copy.start()

    def row_copy(g, zb, cb, way, target):
        layer, r0, size = chunks[g]
        block = zb * CORES + cb
        ref = full.at[layer, :, pl.ds(pl.multiple_of(block * rows + r0, TILE), size), :]
        return pltpu.make_async_remote_copy(
            src_ref=ref,
            dst_ref=ref,
            send_sem=zsend.at[g, zb, way],
            recv_sem=zrecv.at[g, block],
            device_id={"row": target},
            device_id_type=MESH,
        )

    down, up = me - CORES, me + CORES

    def stage_own(g):
        layer, r0, size = chunks[g]
        for head in range(heads):
            for o in range(1, cols):
                col_copy(g, lax.rem(mycol + o, cols), mycol, head).wait_recv()
            own_copy(g, head).wait()
        start = pl.multiple_of(me * rows + r0, TILE)

        @pl.loop(0, heads)
        def _(t):
            full[layer, t, pl.ds(start, size), :] = raws[g][source_ref[t]]

        @pl.loop(0, heads)
        def _(t):
            block = full[layer, t, pl.ds(start, size), :]
            guard[t] = jnp.max(block.reshape(-1, TILE, HDIM), axis=0)

        @pl.when(has_down)
        def _():
            row_copy(g, z, core, 0, down).start()

        @pl.when(has_up)
        def _():
            row_copy(g, z, core, 1, up).start()

        row_copy(g, z, core, 2, partner).start()

    def stage_forward(g):
        for h in range(1, zs):
            @pl.when(z + h < zs)
            def _():
                row_copy(g, z + h, core, 0, down).wait_recv()

                @pl.when(has_down)
                def _():
                    row_copy(g, z + h, core, 0, down).start()

                row_copy(g, z + h, core, 2, partner).start()

            @pl.when(z - h >= 0)
            def _():
                row_copy(g, z - h, core, 1, up).wait_recv()

                @pl.when(has_up)
                def _():
                    row_copy(g, z - h, core, 1, up).start()

                row_copy(g, z - h, core, 2, partner).start()

    def codes_copy(layer):
        return pltpu.make_async_copy(
            cbuf.at[layer % 2], codes_ref.at[layer], outsem.at[1 + layer % 2]
        )

    def checked_copy(layer):
        return pltpu.make_async_copy(
            chk.at[layer % 2], checked_ref.at[layer], outsem.at[3 + layer % 2]
        )

    def compute(layer):
        for g, chunk in enumerate(chunks):
            if chunk[0] == layer:
                @pl.loop(0, zs)
                def _(zb):
                    row_copy(g, zb, 1 - core, 2, partner).wait_recv()
        if layer == 0:
            probe_copy.wait()
        if layer >= 2:
            codes_copy(layer - 2).wait()
            checked_copy(layer - 2).wait()
        slot = layer % 2

        def most(i, acc):
            at = pl.ds(pl.multiple_of(i * KSTEP, KSTEP), KSTEP)
            return tuple(
                jnp.maximum(
                    acc[t],
                    jnp.max(jnp.abs(full[layer, t, at, :]).reshape(-1, TILE, HDIM), axis=0),
                )
                for t in range(heads)
            )

        zero = jnp.zeros((TILE, HDIM), full.dtype)
        best = lax.fori_loop(0, width // KSTEP, most, (zero,) * heads)
        tops = [
            jnp.max(jnp.max(b.astype(jnp.float32), axis=0, keepdims=True), axis=1, keepdims=True)
            for b in best
        ]
        spread = [jnp.broadcast_to(p, (1, HDIM)) for p in tops]
        inverse = [1.0 / ((p + 1e-06) * 0.25) for p in spread]
        here = lax.broadcasted_iota(jnp.int32, peaks_ref.shape, 0) == layer
        lane = lax.broadcasted_iota(jnp.int32, peaks_ref.shape, 1)
        for t in range(heads):
            peaks_ref[...] = jnp.where(here & (lane == t), tops[t], peaks_ref[...])
        for t0 in range(0, heads, 2):
            def step(i, acc):
                at = pl.ds(pl.multiple_of(i * KSTEP, KSTEP), KSTEP)
                both = jnp.concatenate(
                    [
                        (
                            (full[layer, t, at, :].astype(jnp.float32) * 0.25) * inverse[t]
                        ).astype(cbuf.dtype)
                        for t in (t0, t0 + 1)
                    ],
                    axis=1,
                )
                cbuf[slot, at, pl.ds(t0 * HDIM, 2 * HDIM)] = both
                return acc + jnp.dot(pbuf[:, at], both, preferred_element_type=jnp.float32)

            acc = lax.fori_loop(
                0, width // KSTEP, step, jnp.zeros((tokens, 2 * HDIM), jnp.float32)
            )
            scale = jnp.concatenate([spread[t0], spread[t0 + 1]], axis=1)
            chk[slot, :, pl.ds(t0 * HDIM, 2 * HDIM)] = (acc * scale).astype(chk.dtype)
        codes_copy(layer).start()
        checked_copy(layer).start()

    peaks_ref[...] = jnp.zeros_like(peaks_ref)
    total = len(chunks)
    stage_own(0)
    stage_own(1)
    for g in range(total):
        stage_forward(g)
        if g + 2 < total:
            stage_own(g + 2)
        if g + 1 == total or chunks[g + 1][0] != chunks[g][0]:
            compute(chunks[g][0])

    for layer in range(max(layers - 2, 0), layers):
        codes_copy(layer).wait()
        checked_copy(layer).wait()
    for g in range(total):
        for o in range(1, cols):
            for head in range(heads):
                col_copy(g, mycol, lax.rem(mycol + o, cols), head).wait_send()

        @pl.loop(0, zs)
        def _(zb):
            @pl.when(has_down & (zb >= z))
            def _():
                row_copy(g, zb, core, 0, down).wait_send()

            @pl.when(has_up & (zb <= z))
            def _():
                row_copy(g, zb, core, 1, up).wait_send()

            row_copy(g, zb, core, 2, partner).wait_send()


def per_device(train_weight, src_map, tgt_map, probe):
    cols = lax.axis_size("col")
    count = lax.axis_size("row")
    per_col = src_map.shape[0] // cols
    layers, rows, span = train_weight.shape
    tokens, width = probe.shape
    zs = count // CORES
    wanted = lax.dynamic_slice(tgt_map, (lax.axis_index("col") * per_col,), (per_col,))
    source = jnp.argmax(wanted[:, None] == src_map[None, :], axis=1).astype(jnp.int32)
    chunks = chunk_list(layers, rows)
    total = len(chunks)
    anywhere = pl.BlockSpec(memory_space=pl.ANY)
    smem = pl.BlockSpec(memory_space=pltpu.SMEM)
    dtype = train_weight.dtype
    codes, checked, peaks = pl.pallas_call(
        functools.partial(kernel, chunks, zs, cols),
        out_shape=(
            jax.ShapeDtypeStruct((layers, width, span), dtype),
            jax.ShapeDtypeStruct((layers, tokens, span), dtype),
            jax.ShapeDtypeStruct((layers, per_col), jnp.float32),
        ),
        in_specs=[smem, anywhere, anywhere],
        out_specs=(anywhere, anywhere, pl.BlockSpec(memory_space=pltpu.VMEM)),
        scratch_shapes=[
            pltpu.VMEM((layers, per_col, width, HDIM), dtype),
            pltpu.VMEM((2, width, span), dtype),
            pltpu.VMEM((tokens, width), dtype),
            pltpu.VMEM((2, tokens, span), dtype),
            pltpu.VMEM((per_col, TILE, HDIM), dtype),
            pltpu.SemaphoreType.DMA((total, cols, per_col)),
            pltpu.SemaphoreType.DMA((total, cols, per_col)),
            pltpu.SemaphoreType.DMA((total, zs, 3)),
            pltpu.SemaphoreType.DMA((total, count)),
            pltpu.SemaphoreType.DMA((total, per_col)),
            pltpu.SemaphoreType.DMA((5,)),
        ]
        + [pltpu.VMEM((cols * per_col, size, HDIM), dtype) for _, _, size in chunks],
        compiler_params=pltpu.CompilerParams(
            collective_id=0, has_side_effects=True, vmem_limit_bytes=67043328
        ),
    )(source, train_weight, probe)
    return codes, peaks, checked


def solution(mesh):
    in_specs = (P(None, "row", "col"), P(), P(), P("row", None))
    out_specs = (P(None, None, "col"), P(None, "col"), P(None, "row", "col"))
    return jax.shard_map(
        per_device, mesh=mesh, in_specs=in_specs, out_specs=out_specs, check_vma=False
    )
```

time: 346 us -> 208 us (0.60)
  waiting for transfers between devices: 268 us -> 0 us
  Pallas kernels: 0 us -> 187 us
  other arithmetic: 25.1 us -> 1.36 us
  matrix products: 20.3 us -> 0 us
  between operations: 14.1 us -> 0.66 us
    all_gather x2 -> x0, waiting for transfers between devices: 267 us -> none  [the longest x1 169 us: per_device(): lax.all_gather(block_part.reshape(layers, rows_here, per_col * HDIM), 'ro...]
    pallas_call x0 -> x1, Pallas kernels: none -> 187 us  [per_device(): pl.pallas_call(functools.partial(kernel, chunks, zs, cols), out_shape=(ja...]
    dot_general x2 -> x0, matrix products: 20.3 us -> none  [the longest x1 15.2 us: per_device(): jnp.einsum('td,lde->lte', probe, codes, preferred_element_type=jnp.float32)]
    convert_element_type x1 -> x0, other arithmetic: 17.7 us -> none  [per_device(): (joined_four.astype(jnp.float32) / (peaks[:, None, :, None] + 1e-06)).ast...]
    reduce_max x2 -> x0, other arithmetic: 7.46 us -> none  [per_device(): peaks = jnp.max(jnp.abs(joined_four.astype(jnp.float32)), axis=(1, 3))]
    unnamed x10 -> x7, local copies, waits for them, and re-layouts: 13.5 us -> 18.5 us
  transfers between devices with their start and end apart: 2 -> 0, of which waited for: 2 -> 0; matrix products, arithmetic and copies ran while one was open for 0% -> 0% of each run, Pallas kernels for 0% -> 0%
where the time goes in v1:
time: 208 us
  Pallas kernels  187 us (90%)
  local copies, waits for them, and re-layouts  19.3 us (9%)
    pallas_call x1, Pallas kernels, per_device(): pl.pallas_call(functools.partial(kernel, chunks, zs, cols), out_shape=(ja...  187 us
    unnamed x7, local copies, waits for them, and re-layouts  18.5 us

profile of v1, /device:TPU:5, one launch (start us, length us, event | category | flops | bytes accessed | tf_op | source)
XLA Modules:
  0.0 207.9 jit_solution(6642378522341044494)
XLA Ops:
  0.6 0.7 dynamic_slice.3
  1.4 1.4 iota_reduce_fusion
  2.7 186.6 %shard_map.67 = (bf16[4,4608,512]{2,1,0:T(8,128)(2,1)}, bf16[4,512,512]{2,1,0:T(8,128)(2,1)}, f32[4,4]{1,0:T(4,128)}) custom-call(s32[4]{0:T(128)} %get-tuple-element.7.source_ref, bf16[4,576,512]{2,1,0:T(8,128)(2,1)} %w_ref.1, bf16[512,4608]{1,0:T(8,128)(2,1)} %probe_ref.1), custom_call_target="tpu_custom_call" | custom-call | tf_op jit(solution)/shard_map/pallas_call | solution.py:275
  189.3 0.0 copy-start.1
  189.4 0.0 copy-start
  189.4 16.6 %copy.10 = bf16[4,4608,512]{2,1,0:T(8,128)(2,1)} copy(bf16[4,4608,512]{2,1,0:T(8,128)(2,1)} %get-tuple-element.14) | data formatting | bytes 37748736
  206.0 0.0 copy-done.1
  206.0 0.6 copy.11
  206.6 0.0 copy-done
  206.6 1.3 copy.12
Async XLA Ops:
  189.3 16.6 %copy-start.1 = (f32[4,4]{1,0:T(4,128)S(1)}, f32[4,4]{1,0:T(4,128)}, u32[]{:S(2)}) copy-start(f32[4,4]{1,0:T(4,128)} %get-tuple-element.15) | copy-start | bytes 196
  189.4 17.2 %copy-start = (bf16[4,512,512]{2,1,0:T(8,128)(2,1)S(1)}, bf16[4,512,512]{2,1,0:T(8,128)(2,1)}, u32[]{:S(2)}) copy-start(bf16[4,512,512]{2,1,0:T(8,128)(2,1)} %get-tuple-element.16) | copy-start | bytes 6291460

commit v2 on v1

v2 whole, which is shorter than its diff:
```python
import functools

import jax
import jax.numpy as jnp
from jax import lax
from jax.experimental import pallas as pl
from jax.experimental.pallas import tpu as pltpu
from jax.sharding import PartitionSpec as P

HDIM = 128
CORES = 2
TILE = 16
KSTEP = 512
MESH = pl.DeviceIdType.MESH


def pieces_of(rows, most):
    for count in range(most, 0, -1):
        if rows % (TILE * count) == 0:
            return count
    return 1


def piece_list(layers, rows):
    out = []
    for layer in range(layers):
        count = pieces_of(rows, 4 if layer == 0 else (1 if layer == layers - 1 else 2))
        size = rows // count
        for i in range(count):
            out.append((layer, i * size, size))
    return out


def chunk_list(pieces, layers, heads):
    out = []
    for e, (layer, _, _) in enumerate(pieces):
        step = 2 if layer == layers - 1 else heads
        out.extend((e, h0, step) for h0 in range(0, heads, step))
    return out


def kernel(
    pieces, chunks, zs, cols, source_ref, w_ref, probe_ref, codes_ref, checked_ref, peaks_ref,
    full, pbuf, guard,
    csend, crecv, zsend, zrecv, local, probesem, *raws,
):
    layers, heads, width, _ = full.shape
    rows = w_ref.shape[1]
    tokens = pbuf.shape[0]
    me = lax.axis_index("row")
    mycol = lax.axis_index("col")
    z = me // CORES
    core = me % CORES
    partner = z * CORES + (1 - core)
    has_down = z > 0
    has_up = z < zs - 1

    barrier = pltpu.get_barrier_semaphore()
    for o in range(1, cols):
        pl.semaphore_signal(
            barrier, inc=1, device_id={"col": lax.rem(mycol + o, cols)}, device_id_type=MESH
        )
    pl.semaphore_signal(barrier, inc=1, device_id={"row": partner}, device_id_type=MESH)

    @pl.when(has_down)
    def _():
        pl.semaphore_signal(barrier, inc=1, device_id={"row": me - CORES}, device_id_type=MESH)

    @pl.when(has_up)
    def _():
        pl.semaphore_signal(barrier, inc=1, device_id={"row": me + CORES}, device_id_type=MESH)

    pl.semaphore_wait(barrier, cols + has_down.astype(jnp.int32) + has_up.astype(jnp.int32))

    def raw_at(g, owner, head):
        return raws[g].at[owner * heads + head]

    def col_copy(g, owner, target, head):
        layer, r0, size = pieces[g]
        return pltpu.make_async_remote_copy(
            src_ref=w_ref.at[layer, pl.ds(r0, size), pl.ds(head * HDIM, HDIM)],
            dst_ref=raw_at(g, owner, head),
            send_sem=csend.at[g, target, head],
            recv_sem=crecv.at[g, owner, head],
            device_id={"col": target},
            device_id_type=MESH,
        )

    def own_copy(g, head):
        layer, r0, size = pieces[g]
        return pltpu.make_async_copy(
            w_ref.at[layer, pl.ds(r0, size), pl.ds(head * HDIM, HDIM)],
            raw_at(g, mycol, head),
            local.at[g, head],
        )

    for g in range(len(pieces)):
        for head in range(heads):
            for o in range(1, cols):
                col_copy(g, mycol, lax.rem(mycol + o, cols), head).start()
            own_copy(g, head).start()
    probe_copy = pltpu.make_async_copy(probe_ref, pbuf, probesem.at[0])
    probe_copy.start()

    def row_copy(g, zb, cb, way, target):
        piece, h0, hn = chunks[g]
        layer, r0, size = pieces[piece]
        block = zb * CORES + cb
        ref = full.at[layer, pl.ds(h0, hn), pl.ds(pl.multiple_of(block * rows + r0, TILE), size), :]
        return pltpu.make_async_remote_copy(
            src_ref=ref,
            dst_ref=ref,
            send_sem=zsend.at[g, zb, way],
            recv_sem=zrecv.at[g, block],
            device_id={"row": target},
            device_id_type=MESH,
        )

    down, up = me - CORES, me + CORES

    def stage_own(g):
        piece, h0, hn = chunks[g]
        layer, r0, size = pieces[piece]
        for head in range(heads):
            if h0 == 0:
                for o in range(1, cols):
                    col_copy(piece, lax.rem(mycol + o, cols), mycol, head).wait_recv()
                own_copy(piece, head).wait()
        start = pl.multiple_of(me * rows + r0, TILE)

        @pl.loop(h0, h0 + hn)
        def _(t):
            full[layer, t, pl.ds(start, size), :] = raws[piece][source_ref[t]]

        @pl.loop(h0, h0 + hn)
        def _(t):
            block = full[layer, t, pl.ds(start, size), :]
            guard[t] = jnp.max(block.reshape(-1, TILE, HDIM), axis=0)

        @pl.when(has_down)
        def _():
            row_copy(g, z, core, 0, down).start()

        @pl.when(has_up)
        def _():
            row_copy(g, z, core, 1, up).start()

        row_copy(g, z, core, 2, partner).start()

    def stage_forward(g):
        for h in range(1, zs):
            @pl.when(z + h < zs)
            def _():
                row_copy(g, z + h, core, 0, down).wait_recv()

                @pl.when(has_down)
                def _():
                    row_copy(g, z + h, core, 0, down).start()

                row_copy(g, z + h, core, 2, partner).start()

            @pl.when(z - h >= 0)
            def _():
                row_copy(g, z - h, core, 1, up).wait_recv()

                @pl.when(has_up)
                def _():
                    row_copy(g, z - h, core, 1, up).start()

                row_copy(g, z - h, core, 2, partner).start()

    def compute(layer, t0):
        pair = (t0, t0 + 1)

        def most(i, acc):
            at = pl.ds(pl.multiple_of(i * KSTEP, KSTEP), KSTEP)
            return tuple(
                jnp.maximum(
                    acc[t - t0],
                    jnp.max(jnp.abs(full[layer, t, at, :]).reshape(-1, TILE, HDIM), axis=0),
                )
                for t in pair
            )

        zero = jnp.zeros((TILE, HDIM), full.dtype)
        best = lax.fori_loop(0, width // KSTEP, most, (zero,) * 2)
        tops = [
            jnp.max(jnp.max(b.astype(jnp.float32), axis=0, keepdims=True), axis=1, keepdims=True)
            for b in best
        ]
        spread = [jnp.broadcast_to(p, (1, HDIM)) for p in tops]
        inverse = [1.0 / ((p + 1e-06) * 0.25) for p in spread]
        here = lax.broadcasted_iota(jnp.int32, peaks_ref.shape, 0) == layer
        lane = lax.broadcasted_iota(jnp.int32, peaks_ref.shape, 1)
        for t in pair:
            peaks_ref[...] = jnp.where(here & (lane == t), tops[t - t0], peaks_ref[...])

        def step(i, acc):
            at = pl.ds(pl.multiple_of(i * KSTEP, KSTEP), KSTEP)
            both = jnp.concatenate(
                [
                    (
                        (full[layer, t, at, :].astype(jnp.float32) * 0.25) * inverse[t - t0]
                    ).astype(codes_ref.dtype)
                    for t in pair
                ],
                axis=1,
            )
            codes_ref[layer, at, pl.ds(t0 * HDIM, 2 * HDIM)] = both
            return acc + jnp.dot(pbuf[:, at], both, preferred_element_type=jnp.float32)

        acc = lax.fori_loop(0, width // KSTEP, step, jnp.zeros((tokens, 2 * HDIM), jnp.float32))
        scale = jnp.concatenate(spread, axis=1)
        checked_ref[layer, :, pl.ds(t0 * HDIM, 2 * HDIM)] = (acc * scale).astype(
            checked_ref.dtype
        )

    peaks_ref[...] = jnp.zeros_like(peaks_ref)
    total = len(chunks)
    stage_own(0)
    stage_own(1)
    for g in range(total):
        stage_forward(g)
        if g + 2 < total:
            stage_own(g + 2)
        piece, h0, hn = chunks[g]
        layer = pieces[piece][0]
        last = piece + 1 == len(pieces) or pieces[piece + 1][0] != layer
        if last:
            for k, (e, other, _) in enumerate(chunks):
                if pieces[e][0] == layer and other == h0:
                    @pl.loop(0, zs)
                    def _(zb):
                        row_copy(k, zb, 1 - core, 2, partner).wait_recv()
            if layer == 0:
                probe_copy.wait()
            for t0 in range(h0, h0 + hn, 2):
                compute(layer, t0)

    for e in range(len(pieces)):
        for o in range(1, cols):
            for head in range(heads):
                col_copy(e, mycol, lax.rem(mycol + o, cols), head).wait_send()
    for g in range(total):

        @pl.loop(0, zs)
        def _(zb):
            @pl.when(has_down & (zb >= z))
            def _():
                row_copy(g, zb, core, 0, down).wait_send()

            @pl.when(has_up & (zb <= z))
            def _():
                row_copy(g, zb, core, 1, up).wait_send()

            row_copy(g, zb, core, 2, partner).wait_send()


def per_device(train_weight, src_map, tgt_map, probe):
    cols = lax.axis_size("col")
    count = lax.axis_size("row")
    per_col = src_map.shape[0] // cols
    layers, rows, span = train_weight.shape
    tokens, width = probe.shape
    zs = count // CORES
    wanted = lax.dynamic_slice(tgt_map, (lax.axis_index("col") * per_col,), (per_col,))
    source = jnp.argmax(wanted[:, None] == src_map[None, :], axis=1).astype(jnp.int32)
    pieces = piece_list(layers, rows)
    chunks = chunk_list(pieces, layers, per_col)
    total, parts = len(chunks), len(pieces)
    grant = 2 * HDIM * (
        layers * per_col * width + per_col * layers * rows * cols
    ) + 2 * tokens * width + 2**21
    anywhere = pl.BlockSpec(memory_space=pl.ANY)
    smem = pl.BlockSpec(memory_space=pltpu.SMEM)
    dtype = train_weight.dtype
    codes, checked, peaks = pl.pallas_call(
        functools.partial(kernel, pieces, chunks, zs, cols),
        out_shape=(
            pltpu.VMEM((layers, width, span), dtype),
            pltpu.VMEM((layers, tokens, span), dtype),
            jax.ShapeDtypeStruct((layers, per_col), jnp.float32),
        ),
        in_specs=[smem, anywhere, anywhere],
        out_specs=(pl.BlockSpec(memory_space=pltpu.VMEM),) * 3,
        scratch_shapes=[
            pltpu.VMEM((layers, per_col, width, HDIM), dtype),
            pltpu.VMEM((tokens, width), dtype),
            pltpu.VMEM((per_col, TILE, HDIM), dtype),
            pltpu.SemaphoreType.DMA((parts, cols, per_col)),
            pltpu.SemaphoreType.DMA((parts, cols, per_col)),
            pltpu.SemaphoreType.DMA((total, zs, 3)),
            pltpu.SemaphoreType.DMA((total, count)),
            pltpu.SemaphoreType.DMA((parts, per_col)),
            pltpu.SemaphoreType.DMA((1,)),
        ]
        + [pltpu.VMEM((cols * per_col, size, HDIM), dtype) for _, _, size in pieces],
        compiler_params=pltpu.CompilerParams(
            collective_id=0, has_side_effects=True, vmem_limit_bytes=grant
        ),
    )(source, train_weight, probe)
    return codes, peaks, checked


def solution(mesh):
    in_specs = (P(None, "row", "col"), P(), P(), P("row", None))
    out_specs = (P(None, None, "col"), P(None, "col"), P(None, "row", "col"))
    return jax.shard_map(
        per_device, mesh=mesh, in_specs=in_specs, out_specs=out_specs, check_vma=False
    )
```

time: 208 us -> 191 us (0.918)
  local copies, waits for them, and re-layouts: 19.3 us -> 9.48 us
  Pallas kernels: 187 us -> 180 us
    unnamed x7 -> x3, local copies, waits for them, and re-layouts: 18.5 us -> 8.75 us
    pallas_call x1, Pallas kernels: 187 us -> 180 us  [per_device(): pl.pallas_call(functools.partial(kernel, pieces, chunks, zs, cols), out_s...]
where the time goes in v2:
time: 191 us
  Pallas kernels  180 us (94%)
  local copies, waits for them, and re-layouts  9.48 us (5%)
    pallas_call x1, Pallas kernels, per_device(): pl.pallas_call(functools.partial(kernel, pieces, chunks, zs, cols), out_s...  180 us
    unnamed x3, local copies, waits for them, and re-layouts  8.75 us

profile of v2, /device:TPU:5, one launch (start us, length us, event | category | flops | bytes accessed | tf_op | source)
XLA Modules:
  0.0 191.0 jit_solution(5836025221515102666)
XLA Ops:
  0.6 0.7 dynamic_slice.3
  1.4 1.4 iota_reduce_fusion
  2.7 179.5 %shard_map.67 = (bf16[4,4608,512]{2,1,0:T(8,128)(2,1)S(1)}, bf16[4,512,512]{2,1,0:T(8,128)(2,1)S(1)}, f32[4,4]{1,0:T(4,128)S(1)}) custom-call(s32[4]{0:T(128)S(1)} %get-tuple-element.7.source_ref, bf16[4,576,512]{2,1,0:T(8,128)(2,1)} %w_ref.1, bf16[512,4608]{1,0:T(8,128)(2,1)} %probe_ref.1), custom_call_target="tpu_custom_call" | custom-call | tf_op jit(solution)/shard_map/pallas_call | solution.py:277
  182.3 6.9 %copy.10 = bf16[4,4608,512]{2,1,0:T(8,128)(2,1)} copy(bf16[4,4608,512]{2,1,0:T(8,128)(2,1)S(1)} %get-tuple-element.11) | data formatting | bytes 37748736
  189.1 1.3 copy.11
  190.4 0.6 copy.12
